TPU v7x, 8 devices: a whole 2x2x1 slice. The times are simulated.
8 devices in a mesh: dp: 8 (over z, y, x, core).
Axes of the slice: x: 2, y: 2, z: 1, core: 2. Of those that a mesh axis runs over, the one named last changes fastest.
Arguments:
- grad_rows: bfloat16 [8, 25530368], P('dp')
- master: float32 [25530368], P('dp')
- mom_first: float32 [25530368], P('dp')
- mom_second: float32 [25530368], P('dp')
- decay_mask: int32 [25530368], P('dp')
- learn_rate: float32 [1], replicated
Outputs:
- output 1: bfloat16 [25530368], replicated
- output 2: float32 [25530368], P('dp')
- output 3: float32 [25530368], P('dp')
- output 4: float32 [25530368], P('dp')
- output 5: float32 [1], replicated
All inputs are finite; a program needn't handle non-finite values.
Results may differ from a plain program's by a relative error of at most 0.001.
Values are sent between devices in bfloat16 or wider.
A program may use at most 1 GiB of HBM per device.

v0:
```python
import jax
import jax.numpy as jnp
from jax import lax
from jax.sharding import PartitionSpec as P, NamedSharding

BETA_FIRST = 0.9
BETA_SECOND = 0.95
ADAM_EPS = 1e-8
CLIP_EPS = 1e-6
WEIGHT_DECAY = 0.1
ADAM_STEP = 10


def adamw_block(grad_mean, grad_norm, master, mom_first, mom_second, decay_mask, learn_rate):
    clip_coef = jnp.minimum(1.0, 1.0 / (grad_norm + CLIP_EPS))
    clipped = grad_mean * clip_coef
    new_first = BETA_FIRST * mom_first + (1.0 - BETA_FIRST) * clipped
    new_second = BETA_SECOND * mom_second + (1.0 - BETA_SECOND) * clipped * clipped
    step_dir = (new_first / (1.0 - BETA_FIRST ** ADAM_STEP)) / (jnp.sqrt(new_second / (1.0 - BETA_SECOND ** ADAM_STEP)) + ADAM_EPS)
    decay_flag = decay_mask.astype(jnp.float32)
    new_master = master - learn_rate[0] * (step_dir + WEIGHT_DECAY * decay_flag * master)
    return new_master, new_first, new_second


def solution(mesh):
    num_dev = mesh.shape['dp']

    def local_step(grad_row, master, mom_first, mom_second, decay_mask, learn_rate):
        shard_len = master.shape[0]
        grad_parts = grad_row.reshape(num_dev, shard_len)
        received = lax.all_to_all(grad_parts, 'dp', 0, 0, tiled=True)
        grad_mean = jnp.sum(received, axis=0, dtype=jnp.float32) / num_dev
        sq_total = lax.psum(jnp.sum(grad_mean * grad_mean), 'dp')
        grad_norm = jnp.sqrt(sq_total)
        new_master, new_first, new_second = adamw_block(grad_mean, grad_norm, master, mom_first, mom_second, decay_mask, learn_rate)
        params = lax.all_gather(new_master.astype(jnp.bfloat16), 'dp', tiled=True)
        return params, new_master, new_first, new_second, grad_norm.reshape(1)

    return jax.shard_map(local_step, mesh=mesh, in_specs=(P('dp', None), P('dp'), P('dp'), P('dp'), P('dp'), P()), out_specs=(P(), P('dp'), P('dp'), P('dp'), P()), check_vma=False)
```

profile of v0, /device:TPU:0, one launch (start us, length us, event | category | flops | bytes accessed | tf_op | source)
XLA Modules:
  0.0 2556.4 jit_solution(11010697295825855969)
XLA Ops:
  7.2 0.0 all-gather.3.cloned.1.call-start
  7.2 0.5 broadcast.13
  7.7 301.5 %reduce.2 = bf16[8,3191296]{1,0:T(8,128)(2,1)} reduce(bf16[8,1,3191296]{2,1,0:T(2,128)(2,1)} %bitcast.1, bf16[]{:T(256)} %broadcast.13), dimensions={1}, to_apply=%bitcast.1.reduce_sub_computation | reduce | bytes 102121472 | tf_op jit(solution)/shard_map/all_to_all | solution.py:31
  309.2 261.1 %reshape.22 = bf16[8,2,1595648]{2,1,0:T(2,128)(2,1)} reshape(bf16[8,3191296]{1,0:T(8,128)(2,1)} %reduce.2) | data formatting | bytes 102121472
  570.3 565.7 %all_to_all.9 = bf16[8,2,1595648]{2,1,0:T(2,128)(2,1)} all-to-all(bf16[8,2,1595648]{2,1,0:T(2,128)(2,1)} %reshape.22), channel_id=1, replica_groups=mesh['dp'=8] {'dp'}, dimensions={0} | all-to-all | bytes 102121472 | tf_op jit(solution)/shard_map/all_to_all | solution.py:31
  1136.0 164.9 %reshape.23 = bf16[8,1,3191296]{2,1,0:T(2,128)(2,1)} reshape(bf16[8,2,1595648]{2,1,0:T(2,128)(2,1)} %all_to_all.9) | data formatting | bytes 102121472
  1300.9 142.0 %convert_reduce_fusion = f32[3191296]{0:T(1024)} fusion(bf16[8,1,3191296]{2,1,0:T(2,128)(2,1)} %reshape.23), kind=kLoop, calls=%fused_computation | loop fusion | flops 47869440 | bytes 63825920 | tf_op jit(solution)/shard_map/reduce_sum | solution.py:32
  1442.9 7.3 multiply_reduce_fusion
  1450.8 22.9 psum.7
  1474.4 35.6 %fusion.1 = (bf16[3191296]{0:T(1024)(128)(2,1)}, f32[3191296]{0:T(1024)}, f32[3191296]{0:T(1024)}, f32[3191296]{0:T(1024)}) fusion(f32[3191296]{0:T(1024)} %param.7, s32[3191296]{0:T(1024)} %param.10, f32[]{:T(128)} %bitcast.3, f32[3191296]{0:T(1024)} %convert_reduce_fusion, f32[]{:T(128)S(6)} %mul.51, f32[3191296]{0:T(1024)} %param.8, f32[3191296]{0:T(1024)} %param.9), kind=kLoop, calls=%fused_computation.6 | loop fusion | flops 60634624 | bytes 108504072 | tf_op jit(solution)/shard_map/convert_element_type | solution.py:36
  1510.0 62.0 %reshape.19 = bf16[1,1,3191296]{2,1,0:T(2,128)(2,1)} reshape(bf16[3191296]{0:T(1024)(128)(2,1)} %get-tuple-element.5) | data formatting | bytes 12765184
  1571.9 0.0 all-gather.3.cloned.1.call-update
  1572.0 447.7 %all-gather.3.cloned.1.call-done = bf16[8,1,3191296]{2,1,0:T(2,128)(2,1)} async-done(((bf16[1,1,3191296]{2,1,0:T(2,128)(2,1)}), bf16[8,1,3191296]{2,1,0:T(2,128)(2,1)}) %all-gather.3.cloned.1.call-update) | async-done | bytes 51060752 | tf_op jit(solution)/shard_map/all_gather | solution.py:36
  2019.7 301.0 %reduce.1 = bf16[8,3191296]{1,0:T(8,128)(2,1)} reduce(bf16[8,1,3191296]{2,1,0:T(2,128)(2,1)} %all-gather.3.cloned.1.call-done, bf16[]{:T(256)} %constant.26), dimensions={1}, to_apply=%all-gather.reduce_sub_computation | reduce | bytes 102121472 | tf_op jit(solution)/shard_map/all_gather | solution.py:36
  2320.7 227.5 %reshape.20 = bf16[25530368]{0:T(1024)(128)(2,1)} reshape(bf16[8,3191296]{1,0:T(8,128)(2,1)} %reduce.1) | data formatting | bytes 102121472
Async XLA Ops:
  7.2 2012.5 %all-gather.3.cloned.1.call-start = ((), (), s32[]{:S(2)}) async-start(), calls=%async_computation.1 | async-start | bytes 114886656 | tf_op jit(solution)/shard_map/all_gather | solution.py:36
Sparse Core Ops, SparseCore 0:
  1572.1 447.5 all-gather.2
where the time goes:
time: 2570 us; the launch traced here: 2560 us
  other arithmetic  787 us (31%)
  local copies, waits for them, and re-layouts  716 us (28%)
  blocking collectives  589 us (23%)
  waiting for transfers between devices  448 us (17%)
    unnamed x4, local copies, waits for them, and re-layouts  715 us
    all_to_all x1, blocking collectives, local_step(): received = lax.all_to_all(grad_parts, 'dp', 0, 0, tiled=True)  566 us
    all_gather x1, waiting for transfers between devices, local_step(): params = lax.all_gather(new_master.astype(jnp.bfloat16), 'dp', tiled=True)  448 us
    all_to_all x1, other arithmetic, local_step(): received = lax.all_to_all(grad_parts, 'dp', 0, 0, tiled=True)  302 us
    all_gather x1, other arithmetic, local_step(): params = lax.all_gather(new_master.astype(jnp.bfloat16), 'dp', tiled=True)  301 us
    reduce_sum x1, other arithmetic, local_step(): grad_mean = jnp.sum(received, axis=0, dtype=jnp.float32) / num_dev  142 us
  transfers between devices with their start and end apart: 1, of which 1 were waited for; matrix products, arithmetic and copies ran while one was open for 0% of the time, Pallas kernels for 0%

commit v1 on v0

v1 whole, which is shorter than its diff:
```python
import functools

import jax
import jax.numpy as jnp
from jax import lax
from jax.experimental import pallas as pl
from jax.experimental.pallas import tpu as pltpu
from jax.sharding import PartitionSpec as P

BETA_FIRST = 0.9
BETA_SECOND = 0.95
ADAM_EPS = 1e-8
CLIP_EPS = 1e-6
WEIGHT_DECAY = 0.1
ADAM_STEP = 10

MESH = pl.DeviceIdType.MESH
LANES = 128
CHUNK_ROWS = 784
HALF_ROWS = CHUNK_ROWS // 2
SLOTS = 4
GATHER_CHUNKS = 23
ADAM_ROWS = 512


def places():
    me = lax.axis_index("dp")
    core = me % 2
    part = me + 1 - 2 * core
    along_x = me + 2 - 4 * ((me // 2) % 2)
    along_y = me + 4 - 8 * (me // 4)
    return me, part, along_x, along_y


def meet(peers):
    barrier = pltpu.get_barrier_semaphore()
    for peer in peers:
        pl.semaphore_signal(barrier, inc=1, device_id=(peer,), device_id_type=MESH)
    pl.semaphore_wait(barrier, len(peers))


def remote(src, dst, send_sem, recv_sem, device):
    return pltpu.make_async_remote_copy(
        src_ref=src, dst_ref=dst, send_sem=send_sem, recv_sem=recv_sem,
        device_id=(device,), device_id_type=MESH)


def reduce_kernel(shard_rows, grad, g_out, norm_out,
                  own, other, x_send, y_send, x_keep, y_keep, mine, x_recv, y_recv,
                  x_fin, y_fin, x_last, y_last, g_buf, acc, norm_send, norm_recv,
                  own_sem, part_ssem, part_rsem, x_ssem, x_rsem, y_ssem, y_rsem,
                  xf_ssem, xf_rsem, yf_ssem, yf_rsem, g_sem, n_ssem, n_rsem):
    me, part, along_x, along_y = places()
    diag = along_x + along_y - me
    shift = part - me
    blocks = (me, along_x, along_y, diag)
    shard_len = shard_rows * LANES
    full = CHUNK_ROWS * LANES
    chunks = -(-shard_rows // CHUNK_ROWS)
    tail_rows = shard_rows - (chunks - 1) * CHUNK_ROWS
    tail = tail_rows * LANES

    meet((part, along_x, along_y))
    acc[...] = jnp.zeros_like(acc)

    def loads(i, size):
        slot = i % SLOTS
        out = []
        for b, block in enumerate(blocks):
            src = pl.multiple_of(block * shard_len + i * full, LANES)
            out.append(pltpu.make_async_copy(
                grad.at[:, pl.ds(src, size)], own.at[slot, b, :, pl.ds(0, size)], own_sem.at[slot, b]))
        return out

    def swaps(i, size):
        slot = i % SLOTS
        out = []
        for b, block in enumerate(blocks):
            src = pl.multiple_of((block + shift) * shard_len + i * full, LANES)
            out.append(remote(
                grad.at[:, pl.ds(src, size)], other.at[slot, b, :, pl.ds(0, size)],
                part_ssem.at[slot, b], part_rsem.at[slot, b], part))
        return out

    def first_hops(j):
        slot = j % SLOTS
        return (remote(x_send.at[slot], x_recv.at[slot], x_ssem.at[slot], x_rsem.at[slot], along_x),
                remote(y_send.at[slot], y_recv.at[slot], y_ssem.at[slot], y_rsem.at[slot], along_y))

    def last_hops(j):
        slot = j % SLOTS
        return (remote(x_fin.at[slot], x_last.at[slot], xf_ssem.at[slot], xf_rsem.at[slot], along_x),
                remote(y_fin.at[slot], y_last.at[slot], yf_ssem.at[slot], yf_rsem.at[slot], along_y))

    def store_g(j):
        slot = j % 2
        row = pl.multiple_of(j * CHUNK_ROWS, 8)
        return pltpu.make_async_copy(g_buf.at[slot], g_out.at[pl.ds(row, CHUNK_ROWS)], g_sem.at[slot])

    def for_size(i, do):
        @pl.when(i < chunks - 1)
        def _():
            do(full)

        @pl.when(i == chunks - 1)
        def _():
            do(tail)

    def begin(i):
        def do(size):
            for cp in loads(i, size) + swaps(i, size):
                cp.start()
        for_size(i, do)

    def pair_sums(j):
        def do(size):
            for cp in loads(j, size) + swaps(j, size):
                cp.wait()
        for_size(j, do)
        slot = j % SLOTS

        def tile(t, carry):
            for half in range(2):
                row = pl.multiple_of(t * 8, 8)
                col = pl.multiple_of((t + half * (HALF_ROWS // 8)) * 8 * LANES, 8 * LANES)

                def pair(b):
                    a = own[slot, b, :, pl.ds(col, 8 * LANES)].astype(jnp.float32)
                    o = other[slot, b, :, pl.ds(col, 8 * LANES)].astype(jnp.float32)
                    return (a + o).reshape(8, LANES)

                mine[slot, half, pl.ds(row, 8)] = pair(0)
                if half == 0:
                    x_send[slot, 0, pl.ds(row, 8)] = pair(1)
                    y_keep[slot, pl.ds(row, 8)] = pair(2)
                    x_send[slot, 1, pl.ds(row, 8)] = pair(3)
                else:
                    x_keep[slot, pl.ds(row, 8)] = pair(1)
                    y_send[slot, 0, pl.ds(row, 8)] = pair(2)
                    y_send[slot, 1, pl.ds(row, 8)] = pair(3)
            return carry

        lax.fori_loop(0, HALF_ROWS // 8, tile, 0)
        for cp in first_hops(j):
            cp.start()

    def relay(j):
        for cp in first_hops(j):
            cp.wait()
        slot = j % SLOTS
        x_fin[slot] = x_keep[slot] + y_recv[slot, 1]
        y_fin[slot] = y_keep[slot] + x_recv[slot, 1]
        for cp in last_hops(j):
            cp.start()
        mine[slot, 0] = mine[slot, 0] + x_recv[slot, 0]
        mine[slot, 1] = mine[slot, 1] + y_recv[slot, 0]

    def finish(j):
        for cp in last_hops(j):
            cp.wait()
        slot = j % SLOTS
        out = j % 2

        @pl.when(j >= 2)
        def _():
            store_g(j - 2).wait()

        left = shard_rows - j * CHUNK_ROWS
        rows = lax.broadcasted_iota(jnp.int32, (8, LANES), 0)

        def tile(t, total):
            row = pl.multiple_of(t * 8, 8)
            top = (mine[slot, 0, pl.ds(row, 8)] + y_last[slot, pl.ds(row, 8)]) * 0.125
            low = (mine[slot, 1, pl.ds(row, 8)] + x_last[slot, pl.ds(row, 8)]) * 0.125
            g_buf[out, pl.ds(row, 8)] = top
            g_buf[out, pl.ds(pl.multiple_of(HALF_ROWS + t * 8, 8), 8)] = low
            total = total + jnp.where(rows + t * 8 < left, top * top, 0.0)
            return total + jnp.where(rows + (HALF_ROWS + t * 8) < left, low * low, 0.0)

        acc[...] += lax.fori_loop(0, HALF_ROWS // 8, tile, jnp.zeros((8, LANES), jnp.float32))
        store_g(j).start()

    def step(i, carry):
        @pl.when(i < chunks)
        def _():
            begin(i)

        @pl.when((i >= 1) & (i < chunks + 1))
        def _():
            pair_sums(i - 1)

        @pl.when((i >= 2) & (i < chunks + 2))
        def _():
            relay(i - 2)

        @pl.when(i >= 3)
        def _():
            finish(i - 3)

        return carry

    lax.fori_loop(0, chunks + 3, step, 0)
    for k, peer in enumerate((part, along_x, along_y)):
        norm_send[k] = acc[...]
        cp = remote(norm_send.at[k], norm_recv.at[k], n_ssem.at[k], n_rsem.at[k], peer)
        cp.start()
        cp.wait()
        acc[...] = acc[...] + norm_recv[k]
    norm_out[...] = jnp.broadcast_to(jnp.sqrt(jnp.sum(acc[...], keepdims=True)), norm_out.shape)
    store_g(chunks - 2).wait()
    store_g(chunks - 1).wait()


def reduce_scatter(grad_row, shard_rows):
    f32, bf16 = jnp.float32, jnp.bfloat16
    chunks = -(-shard_rows // CHUNK_ROWS)
    vm, dma = pltpu.VMEM, pltpu.SemaphoreType.DMA
    pair = (SLOTS, 2, HALF_ROWS, LANES)
    one = (SLOTS, HALF_ROWS, LANES)
    raw = (SLOTS, 4, 1, CHUNK_ROWS * LANES)
    return pl.pallas_call(
        functools.partial(reduce_kernel, shard_rows),
        out_shape=(jax.ShapeDtypeStruct((chunks * CHUNK_ROWS, LANES), f32),
                   jax.ShapeDtypeStruct((8, LANES), f32)),
        in_specs=[pl.BlockSpec(memory_space=pl.ANY)],
        out_specs=(pl.BlockSpec(memory_space=pl.ANY), pl.BlockSpec(memory_space=pltpu.VMEM)),
        scratch_shapes=[
            vm(raw, bf16), vm(raw, bf16), vm(pair, f32), vm(pair, f32), vm(one, f32), vm(one, f32),
            vm(pair, f32), vm(pair, f32), vm(pair, f32), vm(one, f32), vm(one, f32), vm(one, f32),
            vm(one, f32), vm((2, CHUNK_ROWS, LANES), f32), vm((8, LANES), f32), vm((3, 8, LANES), f32),
            vm((3, 8, LANES), f32),
            dma((SLOTS, 4)), dma((SLOTS, 4)), dma((SLOTS, 4)),
            dma((SLOTS,)), dma((SLOTS,)), dma((SLOTS,)), dma((SLOTS,)),
            dma((SLOTS,)), dma((SLOTS,)), dma((SLOTS,)), dma((SLOTS,)),
            dma((2,)), dma((3,)), dma((3,))],
        compiler_params=pltpu.CompilerParams(collective_id=0, has_side_effects=True,
                                             vmem_limit_bytes=48 << 20),
    )(grad_row)


def adamw_kernel(lr, norm, g, w, m, v, mask, w_out, m_out, v_out, packed):
    coef = jnp.minimum(1.0, 1.0 / (norm[...] + CLIP_EPS))[0:1]
    h = g[...] * coef
    first = BETA_FIRST * m[...] + (1.0 - BETA_FIRST) * h
    second = BETA_SECOND * v[...] + (1.0 - BETA_SECOND) * h * h
    step_dir = (first / (1.0 - BETA_FIRST ** ADAM_STEP)) / (
        jnp.sqrt(second / (1.0 - BETA_SECOND ** ADAM_STEP)) + ADAM_EPS)
    old = w[...]
    new = old - lr[0] * (step_dir + WEIGHT_DECAY * mask[...].astype(jnp.float32) * old)
    w_out[...] = new
    m_out[...] = first
    v_out[...] = second
    packed[...] = new.reshape(packed.shape).astype(packed.dtype)


def adamw(lr, norm, g, w, m, v, mask):
    rows = w.shape[0]
    block = pl.BlockSpec((ADAM_ROWS, LANES), lambda i: (i, 0))
    state = jax.ShapeDtypeStruct((rows, LANES), jnp.float32)
    return pl.pallas_call(
        adamw_kernel,
        grid=(-(-rows // ADAM_ROWS),),
        out_shape=(state, state, state, jax.ShapeDtypeStruct((rows // 4, 4, LANES), jnp.bfloat16)),
        in_specs=[pl.BlockSpec(memory_space=pltpu.SMEM),
                  pl.BlockSpec((8, LANES), lambda i: (0, 0)),
                  block, block, block, block, block],
        out_specs=(block, block, block, pl.BlockSpec((ADAM_ROWS // 4, 4, LANES), lambda i: (i, 0, 0))),
    )(lr, norm, g, w, m, v, mask)


def gather_kernel(new, whole, own, load_sem, keep_sem, x_ssem, y_ssem, xr_ssem, yr_ssem, part_ssem,
                  x_rsem, y_rsem, d_rsem, part_rsem):
    me, part, along_x, along_y = places()
    diag = along_x + along_y - me
    grains = own.shape[0]
    size = grains // GATHER_CHUNKS

    def at(block, q):
        return whole.at[pl.ds(block * grains + q * size, size)]

    def block_at(block):
        return whole.at[pl.ds(block * grains, grains)]

    def to_part(src, block, q, k):
        return remote(src, at(block, q), part_ssem.at[k], part_rsem.at[k], part)

    load = pltpu.make_async_copy(new, own, load_sem)
    load.start()
    meet((part, along_x, along_y))
    load.wait()
    keep = pltpu.make_async_copy(own, block_at(me), keep_sem)
    keep.start()

    def mine(q):
        src = own.at[pl.ds(q * size, size)]
        return (remote(src, at(me, q), x_ssem, x_rsem.at[q], along_x),
                remote(src, at(me, q), y_ssem, y_rsem.at[q], along_y),
                to_part(src, me, q, 0))

    def send(q, carry):
        for cp in mine(q):
            cp.start()
        return carry

    lax.fori_loop(0, GATHER_CHUNKS, send, 0)

    def pass_on(q, carry):
        got = at(along_x, q)
        remote(got, got, x_ssem, x_rsem.at[q], along_x).wait_recv()
        to_part(got, along_x, q, 1).start()

        @pl.when(q % 2 == 0)
        def _():
            remote(got, got, yr_ssem, d_rsem.at[q], along_y).start()

        got = at(along_y, q)
        remote(got, got, y_ssem, y_rsem.at[q], along_y).wait_recv()
        to_part(got, along_y, q, 2).start()

        @pl.when(q % 2 == 1)
        def _():
            remote(got, got, xr_ssem, d_rsem.at[q], along_x).start()

        return carry

    lax.fori_loop(0, GATHER_CHUNKS, pass_on, 0)

    def last(q, carry):
        got = at(diag, q)
        remote(got, got, xr_ssem, d_rsem.at[q], along_x).wait_recv()
        to_part(got, diag, q, 3).start()
        return carry

    lax.fori_loop(0, GATHER_CHUNKS, last, 0)

    evens = size * ((GATHER_CHUNKS + 1) // 2)
    odds = size * (GATHER_CHUNKS // 2)
    remote(own, block_at(me), x_ssem, x_rsem.at[0], along_x).wait_send()
    remote(own, block_at(me), y_ssem, y_rsem.at[0], along_y).wait_send()
    some = whole.at[pl.ds(0, evens)]
    remote(some, some, yr_ssem, d_rsem.at[0], along_y).wait_send()
    some = whole.at[pl.ds(0, odds)]
    remote(some, some, xr_ssem, d_rsem.at[0], along_x).wait_send()
    shift = part - me
    for k, block in enumerate((me, along_x, along_y, diag)):
        cp = remote(block_at(block), block_at(block + shift), part_ssem.at[k], part_rsem.at[k], part)
        cp.wait_send()
        cp.wait_recv()
    keep.wait()


def all_gather(new, num_dev):
    grains = new.shape[0]
    vm, dma = pltpu.VMEM, pltpu.SemaphoreType.DMA
    return pl.pallas_call(
        gather_kernel,
        out_shape=jax.ShapeDtypeStruct((num_dev * grains, 4, LANES), jnp.bfloat16),
        in_specs=[pl.BlockSpec(memory_space=pl.ANY)],
        out_specs=pl.BlockSpec(memory_space=pl.ANY),
        scratch_shapes=[vm((grains, 4, LANES), jnp.bfloat16), dma, dma, dma, dma, dma, dma, dma((4,)),
                        dma((GATHER_CHUNKS,)), dma((GATHER_CHUNKS,)), dma((GATHER_CHUNKS,)), dma((4,))],
        compiler_params=pltpu.CompilerParams(collective_id=1, has_side_effects=True),
    )(new)


def solution(mesh):
    num_dev = mesh.shape["dp"]

    def local_step(grad_row, master, mom_first, mom_second, decay_mask, learn_rate):
        shard_len = master.shape[0]
        rows = shard_len // LANES
        flat = lambda a: a.reshape(rows, LANES)
        g, norm = reduce_scatter(grad_row, rows)
        new_w, new_m, new_v, packed = adamw(
            learn_rate, norm, g, flat(master), flat(mom_first), flat(mom_second), flat(decay_mask))
        params = all_gather(packed, num_dev).reshape(num_dev * shard_len)
        return (params, new_w.reshape(shard_len), new_m.reshape(shard_len), new_v.reshape(shard_len),
                norm[0, 0:1])

    return jax.shard_map(
        local_step, mesh=mesh,
        in_specs=(P("dp", None), P("dp"), P("dp"), P("dp"), P("dp"), P()),
        out_specs=(P(), P("dp"), P("dp"), P("dp"), P()), check_vma=False)
```

time: 2570 us -> 738 us (0.29)
  other arithmetic: 787 us -> 0 us
  Pallas kernels: 0 us -> 700 us
  local copies, waits for them, and re-layouts: 716 us -> 34.8 us
  blocking collectives: 589 us -> 0 us
  waiting for transfers between devices: 448 us -> 0 us
    pallas_call x0 -> x3, Pallas kernels: none -> 700 us  [the longest x1 431 us: reduce_scatter(): pl.pallas_call(functools.partial(reduce_kernel, shard_rows), out_shape=(j...]
    unnamed x4 -> x3, local copies, waits for them, and re-layouts: 715 us -> 34.3 us
    all_to_all x1 -> x0, blocking collectives: 566 us -> none  [local_step(): received = lax.all_to_all(grad_parts, 'dp', 0, 0, tiled=True)]
    all_gather x1 -> x0, waiting for transfers between devices: 448 us -> none  [local_step(): params = lax.all_gather(new_master.astype(jnp.bfloat16), 'dp', tiled=True)]
    all_to_all x1 -> x0, other arithmetic: 302 us -> none  [local_step(): received = lax.all_to_all(grad_parts, 'dp', 0, 0, tiled=True)]
    all_gather x1 -> x0, other arithmetic: 301 us -> none  [local_step(): params = lax.all_gather(new_master.astype(jnp.bfloat16), 'dp', tiled=True)]
    reduce_sum x2 -> x0, other arithmetic: 149 us -> none  [the longest x1 142 us: local_step(): grad_mean = jnp.sum(received, axis=0, dtype=jnp.float32) / num_dev]
    convert_element_type x1 -> x0, other arithmetic: 35.6 us -> none  [local_step(): params = lax.all_gather(new_master.astype(jnp.bfloat16), 'dp', tiled=True)]
  transfers between devices with their start and end apart: 1 -> 0, of which waited for: 1 -> 0; matrix products, arithmetic and copies ran while one was open for 0% -> 0% of each run, Pallas kernels for 0% -> 0%
where the time goes in v1:
time: 738 us; the launch traced here: 737 us
  Pallas kernels  700 us (95%)
  local copies, waits for them, and re-layouts  34.8 us (5%)
    pallas_call x1, Pallas kernels, reduce_scatter(): pl.pallas_call(functools.partial(reduce_kernel, shard_rows), out_shape=(j...  431 us
    pallas_call x1, Pallas kernels, all_gather(): pl.pallas_call(gather_kernel, out_shape=jax.ShapeDtypeStruct((num_dev * g...  213 us
    pallas_call x1, Pallas kernels, adamw(): pl.pallas_call(adamw_kernel, grid=(-(-rows // ADAM_ROWS),), out_shape=(st...  56.4 us
    unnamed x3, local copies, waits for them, and re-layouts  34.3 us

profile of v1, /device:TPU:0, one launch (start us, length us, event | category | flops | bytes accessed | tf_op | source)
XLA Modules:
  0.0 736.5 jit_solution(793702251783237779)
XLA Ops:
  1.3 431.2 %shard_map.101 = (f32[25088,128]{1,0:T(8,128)}, f32[8,128]{1,0:T(8,128)S(1)}) custom-call(bf16[1,25530368]{1,0:T(2,128)(2,1)} %grad.1), custom_call_target="tpu_custom_call" | custom-call | tf_op jit(solution)/shard_map/pallas_call | solution.py:221
  432.5 0.0 copy-start
  432.5 0.5 slice.3
  433.0 0.1 copy-done
  433.1 56.4 %shard_map.102 = (f32[24932,128]{1,0:T(8,128)}, f32[24932,128]{1,0:T(8,128)}, f32[24932,128]{1,0:T(8,128)}, bf16[6233,4,128]{2,1,0:T(4,128)(2,1)}) custom-call(f32[1]{0:T(128)S(6)} %copy.12.lr, f32[8,128]{1,0:T(8,128)} %copy-done, f32[25088,128]{1,0:T(8,128)} %get-tuple-element.12.g, f32[24932,128]{1,0:T(8,128)} %bitcast.10, f32[24932,128]{1,0:T(8,128)} %bitcast.11, ...), custom_call_target="tpu_custom_call" | custom-call | tf_op jit(solution)/shard_map/pallas_call | solution.py:260
  489.5 212.9 %shard_map.103 = bf16[49864,4,128]{2,1,0:T(4,128)(2,1)} custom-call(bf16[6233,4,128]{2,1,0:T(4,128)(2,1)} %get-tuple-element.13.new), custom_call_target="tpu_custom_call" | custom-call | tf_op jit(solution)/shard_map/pallas_call | solution.py:355
  702.4 34.2 %copy.13 = bf16[25530368]{0:T(1024)(128)(2,1)} copy(bf16[25530368]{0:T(1024)(128)(2,1)} %bitcast.9) | data formatting | bytes 102121472
Async XLA Ops:
  432.5 0.6 copy-start

commit v2 on v1

--- a/solution.py
+++ b/solution.py
@@ -16,11 +16,12 @@
 
 MESH = pl.DeviceIdType.MESH
 LANES = 128
-CHUNK_ROWS = 784
+CHUNK_ROWS = 384
 HALF_ROWS = CHUNK_ROWS // 2
 SLOTS = 4
+VMEM_LIMIT = 20 << 20
 GATHER_CHUNKS = 23
-ADAM_ROWS = 512
+ADAM_ROWS = 5 * CHUNK_ROWS
 
 
 def places():
@@ -39,17 +40,21 @@
     pl.semaphore_wait(barrier, len(peers))
 
 
+def stay(array):
+    return pltpu.with_memory_space_constraint(array, pltpu.VMEM)
+
+
 def remote(src, dst, send_sem, recv_sem, device):
     return pltpu.make_async_remote_copy(
         src_ref=src, dst_ref=dst, send_sem=send_sem, recv_sem=recv_sem,
         device_id=(device,), device_id_type=MESH)
 
 
-def reduce_kernel(shard_rows, grad, g_out, norm_out,
+def reduce_kernel(shard_rows, grad, w, m, g_out, w_out, m_out, norm_out,
                   own, other, x_send, y_send, x_keep, y_keep, mine, x_recv, y_recv,
-                  x_fin, y_fin, x_last, y_last, g_buf, acc, norm_send, norm_recv,
+                  x_fin, y_fin, x_last, y_last, acc, norm_recv,
                   own_sem, part_ssem, part_rsem, x_ssem, x_rsem, y_ssem, y_rsem,
-                  xf_ssem, xf_rsem, yf_ssem, yf_rsem, g_sem, n_ssem, n_rsem):
+                  xf_ssem, xf_rsem, yf_ssem, yf_rsem, n_ssem, n_rsem, w_sem, m_sem):
     me, part, along_x, along_y = places()
     diag = along_x + along_y - me
     shift = part - me
@@ -60,7 +65,12 @@
     tail_rows = shard_rows - (chunks - 1) * CHUNK_ROWS
     tail = tail_rows * LANES
 
-    meet((part, along_x, along_y))
+    num_dev = grad.shape[1] // shard_len
+    others = [(me + k) % num_dev for k in range(1, num_dev)]
+    fetches = (pltpu.make_async_copy(w, w_out.at[pl.ds(0, shard_rows)], w_sem),
+               pltpu.make_async_copy(m, m_out.at[pl.ds(0, shard_rows)], m_sem))
+
+    meet(others)
     acc[...] = jnp.zeros_like(acc)
 
     def loads(i, size):
@@ -91,11 +101,6 @@
         slot = j % SLOTS
         return (remote(x_fin.at[slot], x_last.at[slot], xf_ssem.at[slot], xf_rsem.at[slot], along_x),
                 remote(y_fin.at[slot], y_last.at[slot], yf_ssem.at[slot], yf_rsem.at[slot], along_y))
-
-    def store_g(j):
-        slot = j % 2
-        row = pl.multiple_of(j * CHUNK_ROWS, 8)
-        return pltpu.make_async_copy(g_buf.at[slot], g_out.at[pl.ds(row, CHUNK_ROWS)], g_sem.at[slot])
 
     def for_size(i, do):
         @pl.when(i < chunks - 1)
@@ -159,12 +164,7 @@
         for cp in last_hops(j):
             cp.wait()
         slot = j % SLOTS
-        out = j % 2
-
-        @pl.when(j >= 2)
-        def _():
-            store_g(j - 2).wait()
-
+        base = j * CHUNK_ROWS
         left = shard_rows - j * CHUNK_ROWS
         rows = lax.broadcasted_iota(jnp.int32, (8, LANES), 0)
 
@@ -172,13 +172,12 @@
             row = pl.multiple_of(t * 8, 8)
             top = (mine[slot, 0, pl.ds(row, 8)] + y_last[slot, pl.ds(row, 8)]) * 0.125
             low = (mine[slot, 1, pl.ds(row, 8)] + x_last[slot, pl.ds(row, 8)]) * 0.125
-            g_buf[out, pl.ds(row, 8)] = top
-            g_buf[out, pl.ds(pl.multiple_of(HALF_ROWS + t * 8, 8), 8)] = low
+            g_out[pl.ds(pl.multiple_of(base + t * 8, 8), 8)] = top
+            g_out[pl.ds(pl.multiple_of(base + HALF_ROWS + t * 8, 8), 8)] = low
             total = total + jnp.where(rows + t * 8 < left, top * top, 0.0)
             return total + jnp.where(rows + (HALF_ROWS + t * 8) < left, low * low, 0.0)
 
         acc[...] += lax.fori_loop(0, HALF_ROWS // 8, tile, jnp.zeros((8, LANES), jnp.float32))
-        store_g(j).start()
 
     def step(i, carry):
         @pl.when(i < chunks)
@@ -193,52 +192,65 @@
         def _():
             relay(i - 2)
 
-        @pl.when(i >= 3)
-        def _():
-            finish(i - 3)
+        @pl.when(i == 4)
+        def _():
+            for cp in fetches:
+                cp.start()
+
+        @pl.when(i >= 4)
+        def _():
+            finish(i - 4)
 
         return carry
 
-    lax.fori_loop(0, chunks + 3, step, 0)
-    for k, peer in enumerate((part, along_x, along_y)):
-        norm_send[k] = acc[...]
-        cp = remote(norm_send.at[k], norm_recv.at[k], n_ssem.at[k], n_rsem.at[k], peer)
-        cp.start()
+    lax.fori_loop(0, chunks + 4, step, 0)
+    norm_recv[me] = acc[...]
+
+    def shares(peer, k):
+        return remote(acc, norm_recv.at[me], n_ssem.at[k], n_rsem.at[me], peer)
+
+    for k, peer in enumerate(others):
+        shares(peer, k).start()
+    for k, peer in enumerate(others):
+        shares(peer, k).wait_send()
+        remote(acc, norm_recv.at[peer], n_ssem.at[k], n_rsem.at[peer], peer).wait_recv()
+    total = norm_recv[0]
+    for k in range(1, num_dev):
+        total = total + norm_recv[k]
+    for cp in fetches:
         cp.wait()
-        acc[...] = acc[...] + norm_recv[k]
-    norm_out[...] = jnp.broadcast_to(jnp.sqrt(jnp.sum(acc[...], keepdims=True)), norm_out.shape)
-    store_g(chunks - 2).wait()
-    store_g(chunks - 1).wait()
-
-
-def reduce_scatter(grad_row, shard_rows):
+    norm_out[...] = jnp.broadcast_to(jnp.sqrt(jnp.sum(total, keepdims=True)), norm_out.shape)
+
+
+def reduce_scatter(grad_row, w, m, shard_rows, num_dev):
     f32, bf16 = jnp.float32, jnp.bfloat16
     chunks = -(-shard_rows // CHUNK_ROWS)
     vm, dma = pltpu.VMEM, pltpu.SemaphoreType.DMA
     pair = (SLOTS, 2, HALF_ROWS, LANES)
     one = (SLOTS, HALF_ROWS, LANES)
     raw = (SLOTS, 4, 1, CHUNK_ROWS * LANES)
+    state = vm((chunks * CHUNK_ROWS, LANES), f32)
     return pl.pallas_call(
         functools.partial(reduce_kernel, shard_rows),
-        out_shape=(jax.ShapeDtypeStruct((chunks * CHUNK_ROWS, LANES), f32),
-                   jax.ShapeDtypeStruct((8, LANES), f32)),
-        in_specs=[pl.BlockSpec(memory_space=pl.ANY)],
-        out_specs=(pl.BlockSpec(memory_space=pl.ANY), pl.BlockSpec(memory_space=pltpu.VMEM)),
+        out_shape=(state, state, state, jax.ShapeDtypeStruct((8, LANES), f32)),
+        in_specs=[pl.BlockSpec(memory_space=pltpu.HBM)] * 3,
+        out_specs=(pl.BlockSpec(memory_space=vm),) * 4,
         scratch_shapes=[
             vm(raw, bf16), vm(raw, bf16), vm(pair, f32), vm(pair, f32), vm(one, f32), vm(one, f32),
             vm(pair, f32), vm(pair, f32), vm(pair, f32), vm(one, f32), vm(one, f32), vm(one, f32),
-            vm(one, f32), vm((2, CHUNK_ROWS, LANES), f32), vm((8, LANES), f32), vm((3, 8, LANES), f32),
-            vm((3, 8, LANES), f32),
+            vm(one, f32), vm((8, LANES), f32),
+            vm((num_dev, 8, LANES), f32),
             dma((SLOTS, 4)), dma((SLOTS, 4)), dma((SLOTS, 4)),
             dma((SLOTS,)), dma((SLOTS,)), dma((SLOTS,)), dma((SLOTS,)),
             dma((SLOTS,)), dma((SLOTS,)), dma((SLOTS,)), dma((SLOTS,)),
-            dma((2,)), dma((3,)), dma((3,))],
+            dma((num_dev - 1,)), dma((num_dev,)), dma, dma],
         compiler_params=pltpu.CompilerParams(collective_id=0, has_side_effects=True,
-                                             vmem_limit_bytes=48 << 20),
-    )(grad_row)
-
-
-def adamw_kernel(lr, norm, g, w, m, v, mask, w_out, m_out, v_out, packed):
+                                             vmem_limit_bytes=VMEM_LIMIT),
+    )(grad_row, w, m)
+
+
+def adamw_kernel(lr, norm, g, w, m, v, mask, w_out, m_out, v_out, packed, norm_out):
+    norm_out[0] = norm[0, 0]
     coef = jnp.minimum(1.0, 1.0 / (norm[...] + CLIP_EPS))[0:1]
     h = g[...] * coef
     first = BETA_FIRST * m[...] + (1.0 - BETA_FIRST) * h
@@ -254,25 +266,27 @@
 
 
 def adamw(lr, norm, g, w, m, v, mask):
-    rows = w.shape[0]
+    rows = v.shape[0]
     block = pl.BlockSpec((ADAM_ROWS, LANES), lambda i: (i, 0))
     state = jax.ShapeDtypeStruct((rows, LANES), jnp.float32)
     return pl.pallas_call(
         adamw_kernel,
         grid=(-(-rows // ADAM_ROWS),),
-        out_shape=(state, state, state, jax.ShapeDtypeStruct((rows // 4, 4, LANES), jnp.bfloat16)),
+        out_shape=(state, state, state, pltpu.VMEM((g.shape[0] // 4, 4, LANES), jnp.bfloat16),
+                   jax.ShapeDtypeStruct((1,), jnp.float32)),
         in_specs=[pl.BlockSpec(memory_space=pltpu.SMEM),
                   pl.BlockSpec((8, LANES), lambda i: (0, 0)),
                   block, block, block, block, block],
-        out_specs=(block, block, block, pl.BlockSpec((ADAM_ROWS // 4, 4, LANES), lambda i: (i, 0, 0))),
-    )(lr, norm, g, w, m, v, mask)
-
-
-def gather_kernel(new, whole, own, load_sem, keep_sem, x_ssem, y_ssem, xr_ssem, yr_ssem, part_ssem,
+        out_specs=(block, block, block, pl.BlockSpec((ADAM_ROWS // 4, 4, LANES), lambda i: (i, 0, 0)),
+                   pl.BlockSpec(memory_space=pltpu.SMEM)),
+        compiler_params=pltpu.CompilerParams(vmem_limit_bytes=VMEM_LIMIT),
+    )(lr, norm, stay(g), stay(w), stay(m), v, mask)
+
+
+def gather_kernel(grains, own, whole, x_ssem, y_ssem, xr_ssem, yr_ssem, part_ssem,
                   x_rsem, y_rsem, d_rsem, part_rsem):
     me, part, along_x, along_y = places()
     diag = along_x + along_y - me
-    grains = own.shape[0]
     size = grains // GATHER_CHUNKS
 
     def at(block, q):
@@ -284,12 +298,7 @@
     def to_part(src, block, q, k):
         return remote(src, at(block, q), part_ssem.at[k], part_rsem.at[k], part)
 
-    load = pltpu.make_async_copy(new, own, load_sem)
-    load.start()
     meet((part, along_x, along_y))
-    load.wait()
-    keep = pltpu.make_async_copy(own, block_at(me), keep_sem)
-    keep.start()
 
     def mine(q):
         src = own.at[pl.ds(q * size, size)]
@@ -335,8 +344,8 @@
 
     evens = size * ((GATHER_CHUNKS + 1) // 2)
     odds = size * (GATHER_CHUNKS // 2)
-    remote(own, block_at(me), x_ssem, x_rsem.at[0], along_x).wait_send()
-    remote(own, block_at(me), y_ssem, y_rsem.at[0], along_y).wait_send()
+    remote(block_at(me), block_at(me), x_ssem, x_rsem.at[0], along_x).wait_send()
+    remote(block_at(me), block_at(me), y_ssem, y_rsem.at[0], along_y).wait_send()
     some = whole.at[pl.ds(0, evens)]
     remote(some, some, yr_ssem, d_rsem.at[0], along_y).wait_send()
     some = whole.at[pl.ds(0, odds)]
@@ -346,21 +355,46 @@
         cp = remote(block_at(block), block_at(block + shift), part_ssem.at[k], part_rsem.at[k], part)
         cp.wait_send()
         cp.wait_recv()
-    keep.wait()
-
-
-def all_gather(new, num_dev):
-    grains = new.shape[0]
+
+
+def all_gather(packed, grains, num_dev):
     vm, dma = pltpu.VMEM, pltpu.SemaphoreType.DMA
     return pl.pallas_call(
-        gather_kernel,
-        out_shape=jax.ShapeDtypeStruct((num_dev * grains, 4, LANES), jnp.bfloat16),
-        in_specs=[pl.BlockSpec(memory_space=pl.ANY)],
+        functools.partial(gather_kernel, grains),
+        out_shape=vm((num_dev * grains, 4, LANES), jnp.bfloat16),
+        in_specs=[pl.BlockSpec(memory_space=vm)],
+        out_specs=pl.BlockSpec(memory_space=vm),
+        scratch_shapes=[dma, dma, dma, dma, dma((4,)),
+                        dma((GATHER_CHUNKS,)), dma((GATHER_CHUNKS,)), dma((GATHER_CHUNKS,)), dma((4,))],
+        compiler_params=pltpu.CompilerParams(collective_id=1, has_side_effects=True,
+                                             vmem_limit_bytes=1 << 20),
+    )(stay(packed))
+
+
+def store_kernel(grains, own, whole, params, sem):
+    me = lax.axis_index("dp")
+    num_dev = whole.shape[0] // grains
+    copies = []
+    for k in range(num_dev):
+        block = (me + k) % num_dev
+        dst = params.at[pl.ds(block * grains, grains)]
+        src = own.at[pl.ds(0, grains)] if k == 0 else whole.at[pl.ds(block * grains, grains)]
+        copies.append(pltpu.make_async_copy(src, dst, sem.at[k]))
+    for cp in copies:
+        cp.start()
+    for cp in copies:
+        cp.wait()
+
+
+def store(packed, whole, grains, num_dev):
+    return pl.pallas_call(
+        functools.partial(store_kernel, grains),
+        out_shape=jax.ShapeDtypeStruct(whole.shape, whole.dtype),
+        in_specs=[pl.BlockSpec(memory_space=pltpu.VMEM)] * 2,
         out_specs=pl.BlockSpec(memory_space=pl.ANY),
-        scratch_shapes=[vm((grains, 4, LANES), jnp.bfloat16), dma, dma, dma, dma, dma, dma, dma((4,)),
-                        dma((GATHER_CHUNKS,)), dma((GATHER_CHUNKS,)), dma((GATHER_CHUNKS,)), dma((4,))],
-        compiler_params=pltpu.CompilerParams(collective_id=1, has_side_effects=True),
-    )(new)
+        scratch_shapes=[pltpu.SemaphoreType.DMA((num_dev,))],
+        compiler_params=pltpu.CompilerParams(vmem_limit_bytes=1 << 20),
+    )(stay(packed), stay(whole))
 
 
 def solution(mesh):
@@ -370,12 +404,13 @@
         shard_len = master.shape[0]
         rows = shard_len // LANES
         flat = lambda a: a.reshape(rows, LANES)
-        g, norm = reduce_scatter(grad_row, rows)
-        new_w, new_m, new_v, packed = adamw(
-            learn_rate, norm, g, flat(master), flat(mom_first), flat(mom_second), flat(decay_mask))
-        params = all_gather(packed, num_dev).reshape(num_dev * shard_len)
+        g, w, m, norm = reduce_scatter(grad_row, flat(master), flat(mom_first), rows, num_dev)
+        new_w, new_m, new_v, packed, grad_norm = adamw(
+            learn_rate, norm, g, w, m, flat(mom_second), flat(decay_mask))
+        whole = all_gather(packed, rows // 4, num_dev)
+        params = store(packed, whole, rows // 4, num_dev).reshape(num_dev * shard_len)
         return (params, new_w.reshape(shard_len), new_m.reshape(shard_len), new_v.reshape(shard_len),
-                norm[0, 0:1])
+                grad_norm)
 
     return jax.shard_map(
         local_step, mesh=mesh,

time: 738 us -> 689 us (0.934)
  local copies, waits for them, and re-layouts: 34.8 us -> 0 us
  Pallas kernels: 700 us -> 687 us
    unnamed x3 -> x0, local copies, waits for them, and re-layouts: 34.3 us -> none
    pallas_call x1, Pallas kernels: 56.4 us -> 33.3 us  [adamw(): pl.pallas_call(adamw_kernel, grid=(-(-rows // ADAM_ROWS),), out_shape=(st...]
    pallas_call x2 -> x3, Pallas kernels: 644 us -> 654 us  [the longest x1 425 us: reduce_scatter(): pl.pallas_call(functools.partial(reduce_kernel, shard_rows), out_shape=(s...]
where the time goes in v2:
time: 689 us
  Pallas kernels  687 us (100%)
    pallas_call x1, Pallas kernels, reduce_scatter(): pl.pallas_call(functools.partial(reduce_kernel, shard_rows), out_shape=(s...  425 us
    pallas_call x1, Pallas kernels, all_gather(): pl.pallas_call(functools.partial(gather_kernel, grains), out_shape=vm((nu...  213 us
    pallas_call x1, Pallas kernels, adamw(): pl.pallas_call(adamw_kernel, grid=(-(-rows // ADAM_ROWS),), out_shape=(st...  33.3 us
    pallas_call x1, Pallas kernels, store(): pl.pallas_call(functools.partial(store_kernel, grains), out_shape=jax.Sha...  16.4 us

profile of v2, /device:TPU:0, one launch (start us, length us, event | category | flops | bytes accessed | tf_op | source)
XLA Modules:
  0.0 688.6 jit_solution(10641904920269096361)
XLA Ops:
  1.3 424.7 %shard_map.101 = (f32[24960,128]{1,0:T(8,128)S(1)}, f32[24960,128]{1,0:T(8,128)S(1)}, f32[24960,128]{1,0:T(8,128)S(1)}, f32[8,128]{1,0:T(8,128)}) custom-call(bf16[1,25530368]{1,0:T(2,128)(2,1)} %grad.1, f32[24932,128]{1,0:T(8,128)} %bitcast.9, f32[24932,128]{1,0:T(8,128)} %bitcast.10), custom_call_target="tpu_custom_call" | custom-call | tf_op jit(solution)/shard_map/pallas_call | solution.py:233
  426.0 33.3 %shard_map.102 = (f32[24932,128]{1,0:T(8,128)}, f32[24932,128]{1,0:T(8,128)}, f32[24932,128]{1,0:T(8,128)}, bf16[6240,4,128]{2,1,0:T(4,128)(2,1)S(1)}, f32[1]{0:T(128)}) custom-call(f32[1]{0:T(128)S(6)} %copy.11.lr, f32[8,128]{1,0:T(8,128)} %get-tuple-element.14.norm, f32[24960,128]{1,0:T(8,128)S(1)} %get-tuple-element.15.g, ...), custom_call_target="tpu_custom_call" | custom-call | tf_op jit(solution)/shard_map/pallas_call | solution.py:272
  459.3 212.9 %shard_map.103.whole = bf16[49864,4,128]{2,1,0:T(4,128)(2,1)S(1)} custom-call(bf16[6240,4,128]{2,1,0:T(4,128)(2,1)S(1)} %get-tuple-element.18.own), custom_call_target="tpu_custom_call" | custom-call | tf_op jit(solution)/shard_map/pallas_call | solution.py:362
  672.2 16.4 %shard_map.104 = bf16[49864,4,128]{2,1,0:T(4,128)(2,1)} custom-call(bf16[6240,4,128]{2,1,0:T(4,128)(2,1)S(1)} %get-tuple-element.18.own, bf16[49864,4,128]{2,1,0:T(4,128)(2,1)S(1)} %shard_map.103.whole), custom_call_target="tpu_custom_call" | custom-call | tf_op jit(solution)/shard_map/pallas_call | solution.py:390

commit v3 on v2

--- a/solution.py
+++ b/solution.py
@@ -22,6 +22,7 @@
 VMEM_LIMIT = 20 << 20
 GATHER_CHUNKS = 23
 ADAM_ROWS = 5 * CHUNK_ROWS
+TILE_ROWS = 128
 
 
 def places():
@@ -251,18 +252,26 @@
 
 def adamw_kernel(lr, norm, g, w, m, v, mask, w_out, m_out, v_out, packed, norm_out):
     norm_out[0] = norm[0, 0]
-    coef = jnp.minimum(1.0, 1.0 / (norm[...] + CLIP_EPS))[0:1]
-    h = g[...] * coef
-    first = BETA_FIRST * m[...] + (1.0 - BETA_FIRST) * h
-    second = BETA_SECOND * v[...] + (1.0 - BETA_SECOND) * h * h
-    step_dir = (first / (1.0 - BETA_FIRST ** ADAM_STEP)) / (
-        jnp.sqrt(second / (1.0 - BETA_SECOND ** ADAM_STEP)) + ADAM_EPS)
-    old = w[...]
-    new = old - lr[0] * (step_dir + WEIGHT_DECAY * mask[...].astype(jnp.float32) * old)
-    w_out[...] = new
-    m_out[...] = first
-    v_out[...] = second
-    packed[...] = new.reshape(packed.shape).astype(packed.dtype)
+    coef = jnp.minimum(1.0, 1.0 / (norm[0:1] + CLIP_EPS))
+    rate = lr[0]
+
+    def tile(t, carry):
+        at = pl.ds(pl.multiple_of(t * TILE_ROWS, TILE_ROWS), TILE_ROWS)
+        h = g[at] * coef
+        first = BETA_FIRST * m[at] + (1.0 - BETA_FIRST) * h
+        second = BETA_SECOND * v[at] + (1.0 - BETA_SECOND) * h * h
+        step_dir = (first * (1.0 / (1.0 - BETA_FIRST ** ADAM_STEP))) / (
+            jnp.sqrt(second * (1.0 / (1.0 - BETA_SECOND ** ADAM_STEP))) + ADAM_EPS)
+        old = w[at]
+        new = old - rate * (step_dir + WEIGHT_DECAY * mask[at].astype(jnp.float32) * old)
+        w_out[at] = new
+        m_out[at] = first
+        v_out[at] = second
+        grains = TILE_ROWS // 4
+        packed[pl.ds(pl.multiple_of(t * grains, grains), grains)] = new.reshape(grains, 4, LANES).astype(packed.dtype)
+        return carry
+
+    lax.fori_loop(0, ADAM_ROWS // TILE_ROWS, tile, 0)
 
 
 def adamw(lr, norm, g, w, m, v, mask):

time: 689 us -> 685 us (level)
  no operation moved by 1% of the time
where the time goes in v3:
time: 685 us
  Pallas kernels  684 us (100%)
    pallas_call x1, Pallas kernels, reduce_scatter(): pl.pallas_call(functools.partial(reduce_kernel, shard_rows), out_shape=(s...  425 us
    pallas_call x1, Pallas kernels, all_gather(): pl.pallas_call(functools.partial(gather_kernel, grains), out_shape=vm((nu...  213 us
    pallas_call x1, Pallas kernels, adamw(): pl.pallas_call(adamw_kernel, grid=(-(-rows // ADAM_ROWS),), out_shape=(st...  29.6 us
    pallas_call x1, Pallas kernels, store(): pl.pallas_call(functools.partial(store_kernel, grains), out_shape=jax.Sha...  16.4 us

profile of v3, /device:TPU:0, one launch (start us, length us, event | category | flops | bytes accessed | tf_op | source)
XLA Modules:
  0.0 684.9 jit_solution(5939416052599003104)
XLA Ops:
  1.3 424.7 %shard_map.101 = (f32[24960,128]{1,0:T(8,128)S(1)}, f32[24960,128]{1,0:T(8,128)S(1)}, f32[24960,128]{1,0:T(8,128)S(1)}, f32[8,128]{1,0:T(8,128)}) custom-call(bf16[1,25530368]{1,0:T(2,128)(2,1)} %grad.1, f32[24932,128]{1,0:T(8,128)} %bitcast.9, f32[24932,128]{1,0:T(8,128)} %bitcast.10), custom_call_target="tpu_custom_call" | custom-call | tf_op jit(solution)/shard_map/pallas_call | solution.py:234
  426.0 29.6 %shard_map.102 = (f32[24932,128]{1,0:T(8,128)}, f32[24932,128]{1,0:T(8,128)}, f32[24932,128]{1,0:T(8,128)}, bf16[6240,4,128]{2,1,0:T(4,128)(2,1)S(1)}, f32[1]{0:T(128)}) custom-call(f32[1]{0:T(128)S(6)} %copy.11.lr, f32[8,128]{1,0:T(8,128)} %get-tuple-element.14.norm, f32[24960,128]{1,0:T(8,128)S(1)} %get-tuple-element.15.g, ...), custom_call_target="tpu_custom_call" | custom-call | tf_op jit(solution)/shard_map/pallas_call | solution.py:281
  455.6 212.9 %shard_map.103.whole = bf16[49864,4,128]{2,1,0:T(4,128)(2,1)S(1)} custom-call(bf16[6240,4,128]{2,1,0:T(4,128)(2,1)S(1)} %get-tuple-element.18.own), custom_call_target="tpu_custom_call" | custom-call | tf_op jit(solution)/shard_map/pallas_call | solution.py:371
  668.5 16.4 %shard_map.104 = bf16[49864,4,128]{2,1,0:T(4,128)(2,1)} custom-call(bf16[6240,4,128]{2,1,0:T(4,128)(2,1)S(1)} %get-tuple-element.18.own, bf16[49864,4,128]{2,1,0:T(4,128)(2,1)S(1)} %shard_map.103.whole), custom_call_target="tpu_custom_call" | custom-call | tf_op jit(solution)/shard_map/pallas_call | solution.py:399
